TPU v7x, 32 devices: a whole 2x2x4 slice. The times are simulated.
32 devices in a mesh: copies: 2 (over y), grid: 4 (over z), slab: 4 (over x, core).
Axes of the slice: x: 2, y: 2, z: 4, core: 2. Of those that a mesh axis runs over, the one named last changes fastest.
Arguments:
- field: float32 [8, 128, 64, 128], P(('copies', 'grid'), 'slab'), parts along dimension 0, may hold values from -6 to 6
- levels: int32 [8, 5], P(('copies', 'grid')), parts along dimension 0, may hold values from 1 to 3
- owner: int32 [256], P('copies'), parts along dimension 0, may hold values from 0 to 127, each once
Outputs:
- combined: float32 [256, 64, 128], P(('copies', 'grid'), 'slab'), parts along dimension 0
There are 2 independent parts, one for each index of `copies`. A program takes and returns all parts, laid end to end along the dimension named above; each array names one. Nothing has to cross between parts.
All inputs are finite; a program needn't handle non-finite values.
Results may differ from a plain program's by a relative error of at most 0.0003.
Values sent between devices are 32-bit elements; how exact they have to be, the bound alone decides.
A program may use at most 64 MiB of HBM per device.

v0:
```python
import math

import jax
import jax.numpy as jnp
import numpy as np
from jax import lax
from jax.sharding import PartitionSpec as P

N0 = 128
N1 = 2
N2 = 8
N3 = 4
N4 = 128
STEPS = 4
Q = 64


ADVECT = 0.08
DIFFUSE = 0.03


def extended_2(value, sides, width):
    for axis, dim in sides:
        count, length = (lax.axis_size(axis), value.shape[dim])
        up = [(i, (i + 1) % count) for i in range(count)]
        down = [(j, i) for i, j in up]
        last = lax.slice_in_dim(value, length - width, length, axis=dim)
        first = lax.slice_in_dim(value, 0, width, axis=dim)
        before = lax.ppermute(last, axis, up)
        after = lax.ppermute(first, axis, down)
        value = jnp.concatenate([before, value, after], axis=dim)
    return value


def build_tables(count):
    depth = count.bit_length() - 1
    matrix = np.eye(count)
    inverse = np.zeros((count, count))
    inverse[0, 0] = 1.0
    level_rows = np.zeros(count, np.int32)
    for index in range(1, count):
        zeros = (index & -index).bit_length() - 1
        spacing = 1 << zeros
        matrix[index, index - spacing] -= 0.5
        matrix[index, (index + spacing) % count] -= 0.5
        level_rows[index] = depth - zeros
    for zeros in range(depth - 1, -1, -1):
        spacing = 1 << zeros
        for index in range(spacing, count, 2 * spacing):
            inverse[index] = 0.5 * (inverse[index - spacing] + inverse[(index + spacing) % count])
            inverse[index, index] += 1.0
    return (matrix.astype(np.float32), inverse.astype(np.float32), level_rows)


def advance(extended, scales, padded):
    length = extended.shape[padded] - 2
    centre = lax.slice_in_dim(extended, 1, length + 1, axis=padded)
    speed = 1.0 + 0.5 * jnp.tanh(centre)
    change = jnp.zeros_like(centre)
    for axis in range(5):
        if axis == padded:
            back = lax.slice_in_dim(extended, 0, length, axis=padded)
            ahead = lax.slice_in_dim(extended, 2, length + 2, axis=padded)
        else:
            back = jnp.roll(centre, 1, axis)
            ahead = jnp.roll(centre, -1, axis)
        change = (
            change
            - ADVECT * scales[axis] * speed * (centre - back)
            + DIFFUSE * scales[axis] ** 2 * (ahead - 2.0 * centre + back)
        )
    return centre + change


def regroup_rows(stepped):
    return lax.all_to_all(stepped, "slab", split_axis=1, concat_axis=0, tiled=True)


def local(field, levels, owner):
    matrix, inverse, level_rows = build_tables(N0)
    matrix = jnp.asarray(matrix)
    inverse = jnp.asarray(inverse)
    depth = N0.bit_length() - 1
    level_vec = levels[0]
    scales = jnp.exp2(level_vec.astype(jnp.float32)) / 8.0
    weight = jnp.where(jnp.sum(level_vec) % 2 == 0, 1.0, -1.0).astype(jnp.float32) / math.sqrt(
        lax.axis_size("grid")
    )
    keep = (jnp.asarray(level_rows) <= depth - 3 + level_vec[0]).astype(jnp.float32)[:, None, None]

    def evolve_rows(state):
        rows = state.shape[0]
        grid5 = state.reshape(rows, N1, N2, N3, N4)
        for step in range(STEPS):
            extended = extended_2(grid5, (("slab", 0),), 1)
            grid5 = advance(extended, scales, 0)
        return grid5.reshape(rows, Q, N4)

    def hierarchise(whole):
        hier = jnp.dot(matrix, whole.reshape(N0, -1), precision=lax.Precision.HIGHEST)
        return weight * keep * hier.reshape(whole.shape)

    def reduce_terms(terms):
        return lax.psum_scatter(terms[owner], "grid", scatter_dimension=0, tiled=True)

    stepped = evolve_rows(field[0])
    summed = reduce_terms(hierarchise(regroup_rows(stepped)))
    ordered = lax.all_gather(summed, "grid", axis=0, tiled=True)
    position = jnp.zeros((N0,), jnp.int32).at[owner].set(jnp.arange(N0, dtype=jnp.int32))
    combined = ordered[position]
    masked = (keep * combined).reshape(N0, -1)
    nodal = jnp.dot(inverse, masked, precision=lax.Precision.HIGHEST).reshape(combined.shape)
    state = lax.all_to_all(nodal, "slab", split_axis=0, concat_axis=1, tiled=True)
    stepped = evolve_rows(state)
    summed = reduce_terms(hierarchise(regroup_rows(stepped)))
    return summed


def solution(mesh):
    in_specs = (P(("copies", "grid"), "slab", None, None), P(("copies", "grid"), None), P("copies"))
    out_specs = P(("copies", "grid"), "slab", None)
    return jax.shard_map(local, mesh=mesh, in_specs=in_specs, out_specs=out_specs, check_vma=False)
```

profile of v0, /device:TPU:0, one launch (start us, length us, event | category | flops | bytes accessed | tf_op | source)
XLA Modules:
  0.0 231.8 jit_solution(14325692422374188094)
XLA Ops:
  7.3 2.4 %collective-permute-start.1 = (f32[1,2,8,4,128]{4,0,3,2,1:T(1,128)S(1)}, f32[1,2,8,4,128]{4,0,3,2,1:T(1,128)S(1)}, u32[]{:S(2)}, u32[]{:S(2)}) collective-permute-start(f32[1,2,8,4,128]{4,0,3,2,1:T(1,128)S(1)} %bitcast.80), channel_id=1, source_target_pairs={{1,0},{2,1},{3,2},{0,3},{5,4},{6,5},{7,6},{4,7},{9,8},{10,9},{11,1... | collective-permute-start | bytes 98312 | tf_op jit(solution)/shard_map/ppermute | solution.py:30
  9.7 1.8 copy.37
  23.8 2.3 %fusion.8 = f32[32,2,8,4,128]{4,0,3,2,1:T(8,128)S(1)} fusion(f32[32,2,8,4,128]{4,0,3,2,1:T(8,128)S(1)} %copy.37, f32[1,2,8,4,128]{4,0,3,2,1:T(1,128)S(1)} %collective-permute-done.1, f32[1,2,8,4,128]{4,0,3,2,1:T(1,128)S(1)} %collective-permute-done, f32[32,2,1,4,128]{4,0,3,2,1:T(8,128)S(1)} %get-tuple-element.120, ...), kind=kLoop, calls=%fused_computation.23 | loop fusion | flops 13893632 | bytes 9502760 | tf_op jit(solution)/shard_map/add | solution.py:72
  27.6 1.8 collective-permute-start.3
  29.4 1.7 collective-permute-done.3
  31.1 1.6 collective-permute-done.2
  32.7 2.3 fusion.17
  37.1 1.6 collective-permute-done.5
  38.7 1.7 collective-permute-done.4
  40.4 2.3 fusion.26
  44.7 1.3 collective-permute-done.7
  46.0 1.7 collective-permute-done.6
  47.8 3.1 %fusion.35 = f32[32,2,8,4,128]{4,0,3,2,1:T(8,128)} fusion(f32[32,2,8,4,128]{4,0,3,2,1:T(8,128)S(1)} %fusion.26, f32[1,2,8,4,128]{4,0,3,2,1:T(1,128)S(1)} %collective-permute-done.7, f32[1,2,8,4,128]{4,0,3,2,1:T(1,128)S(1)} %collective-permute-done.6, f32[32,2,1,4,128]{4,0,3,2,1:T(8,128)S(1)} %get-tuple-element.72, ...), kind=kLoop, calls=%fused_computation.50 | loop fusion | flops 13893632 | bytes 9502760 | tf_op jit(solution)/shard_map/add | solution.py:72
  50.8 3.5 %all-to-all-start = ((f32[32,64,128]{2,0,1:T(8,128)}), f32[32,64,128]{2,0,1:T(8,128)S(1)}, u32[]{:S(2)}, u32[]{:S(2)}) async-start(f32[32,64,128]{2,0,1:T(8,128)} %bitcast.16), calls=%async_computation | async-start | bytes 2097152 | tf_op jit(solution)/shard_map/all_to_all | solution.py:76
  58.5 10.3 %all-to-all-done = f32[32,64,128]{2,0,1:T(8,128)S(1)} async-done(((f32[32,64,128]{2,0,1:T(8,128)}), f32[32,64,128]{2,0,1:T(8,128)S(1)}, u32[]{:S(2)}, u32[]{:S(2)}) %all-to-all-start) | async-done | bytes 1048608 | tf_op jit(solution)/shard_map/all_to_all | solution.py:76
  71.3 1.7 gather_fusion
  73.1 27.7 %reduce-scatter.3.cloned.1.call-done = f32[32,16,128]{2,1,0:T(8,128)} async-done(((f32[128,16,128]{2,1,0:T(8,128)}), f32[32,16,128]{2,1,0:T(8,128)}) %reduce-scatter.3.cloned.1.call-update) | async-done | bytes 262160 | tf_op jit(solution)/shard_map/reduce_scatter | solution.py:104
  102.0 27.0 %all-gather.2.cloned.1.call-done = f32[128,16,128]{2,1,0:T(8,128)} async-done(((f32[32,16,128]{2,1,0:T(8,128)}), f32[128,16,128]{2,1,0:T(8,128)}) %all-gather.2.cloned.1.call-update) | async-done | bytes 1048592 | tf_op jit(solution)/shard_map/all_gather | solution.py:108
  128.9 1.9 gather_fusion.1
  130.8 1.3 convolution_bitcast_fusion.1
  132.3 17.0 %all_to_all.45 = f32[128,16,128]{2,1,0:T(8,128)S(1)} all-to-all(f32[128,16,128]{2,1,0:T(8,128)S(1)} %bitcast.75), channel_id=1, replica_groups=mesh['copies'=2,'grid'=4,'slab'=4] {'slab'}, dimensions={0} | all-to-all | bytes 2097152 | tf_op jit(solution)/shard_map/all_to_all | solution.py:113
  152.6 1.8 collective-permute-done.8
  154.4 2.3 fusion.44
  159.8 1.8 collective-permute-done.10
  161.6 2.3 fusion.53
  166.9 2.0 collective-permute-done.12
  169.0 2.3 fusion.62
  174.3 1.8 collective-permute-done.14
  176.1 2.3 fusion.71
  178.4 16.9 %all_to_all.46 = f32[32,64,128]{2,0,1:T(8,128)S(1)} all-to-all(f32[32,64,128]{2,0,1:T(8,128)S(1)} %bitcast.77), channel_id=1, replica_groups=mesh['copies'=2,'grid'=4,'slab'=4] {'slab'}, dimensions={1} | all-to-all | bytes 2097152 | tf_op jit(solution)/shard_map/all_to_all | solution.py:76
  197.6 1.7 gather_fusion.2
  199.3 25.9 %reduce-scatter.5.cloned.1.call-done = f32[32,16,128]{2,1,0:T(8,128)} async-done(((f32[128,16,128]{2,1,0:T(8,128)}), f32[32,16,128]{2,1,0:T(8,128)}) %reduce-scatter.5.cloned.1.call-update) | async-done | bytes 262160 | tf_op jit(solution)/shard_map/reduce_scatter | solution.py:104
  (121 shorter events, 29.2 us)
Async XLA Ops:
  7.3 16.5 %collective-permute-start.1 = (f32[1,2,8,4,128]{4,0,3,2,1:T(1,128)S(1)}, f32[1,2,8,4,128]{4,0,3,2,1:T(1,128)S(1)}, u32[]{:S(2)}, u32[]{:S(2)}) collective-permute-start(f32[1,2,8,4,128]{4,0,3,2,1:T(1,128)S(1)} %bitcast.80), channel_id=1, source_target_pairs={{1,0},{2,1},{3,2},{0,3},{5,4},{6,5},{7,6},{4,7},{9,8},{10,9},{11,1... | collective-permute-start | bytes 98312 | tf_op jit(solution)/shard_map/ppermute | solution.py:30
  9.7 14.1 %collective-permute-start = (f32[1,2,8,4,128]{4,0,3,2,1:T(1,128)S(1)}, f32[1,2,8,4,128]{4,0,3,2,1:T(1,128)S(1)}, u32[]{:S(2)}, u32[]{:S(2)}) collective-permute-start(f32[1,2,8,4,128]{4,0,3,2,1:T(1,128)S(1)} %bitcast.79), channel_id=1, source_target_pairs={{0,1},{1,2},{2,3},{3,0},{4,5},{5,6},{6,7},{7,4},{8,9},{9,10},{10,1... | collective-permute-start | bytes 98312 | tf_op jit(solution)/shard_map/ppermute | solution.py:29
  12.8 0.7 copy-start.3
  27.6 3.5 %collective-permute-start.3 = (f32[1,2,8,4,128]{4,0,3,2,1:T(1,128)S(1)}, f32[1,2,8,4,128]{4,0,3,2,1:T(1,128)S(1)}, u32[]{:S(2)}, u32[]{:S(2)}) collective-permute-start(f32[1,2,8,4,128]{4,0,3,2,1:T(1,128)S(1)} %get-tuple-element.116), channel_id=1, source_target_pairs={{1,0},{2,1},{3,2},{0,3},{5,4},{6,5},{7,6},{4,7},{9,8},{10,9},{11,1... | collective-permute-start | bytes 98312 | tf_op jit(solution)/shard_map/ppermute | solution.py:30
  29.4 3.3 %collective-permute-start.2 = (f32[1,2,8,4,128]{4,0,3,2,1:T(1,128)S(1)}, f32[1,2,8,4,128]{4,0,3,2,1:T(1,128)S(1)}, u32[]{:S(2)}, u32[]{:S(2)}) collective-permute-start(f32[1,2,8,4,128]{4,0,3,2,1:T(1,128)S(1)} %get-tuple-element.115), channel_id=1, source_target_pairs={{0,1},{1,2},{2,3},{3,0},{4,5},{5,6},{6,7},{7,4},{8,9},{9,10},{10,1... | collective-permute-start | bytes 98312 | tf_op jit(solution)/shard_map/ppermute | solution.py:29
  36.4 2.3 collective-permute-start.5
  37.1 3.3 %collective-permute-start.4 = (f32[1,2,8,4,128]{4,0,3,2,1:T(1,128)S(1)}, f32[1,2,8,4,128]{4,0,3,2,1:T(1,128)S(1)}, u32[]{:S(2)}, u32[]{:S(2)}) collective-permute-start(f32[1,2,8,4,128]{4,0,3,2,1:T(1,128)S(1)} %get-tuple-element.99), channel_id=1, source_target_pairs={{0,1},{1,2},{2,3},{3,0},{4,5},{5,6},{6,7},{7,4},{8,9},{9,10},{10,1... | collective-permute-start | bytes 98312 | tf_op jit(solution)/shard_map/ppermute | solution.py:29
  44.1 1.9 collective-permute-start.7
  44.4 3.3 %collective-permute-start.6 = (f32[1,2,8,4,128]{4,0,3,2,1:T(1,128)S(1)}, f32[1,2,8,4,128]{4,0,3,2,1:T(1,128)S(1)}, u32[]{:S(2)}, u32[]{:S(2)}) collective-permute-start(f32[1,2,8,4,128]{4,0,3,2,1:T(1,128)S(1)} %get-tuple-element.83), channel_id=1, source_target_pairs={{0,1},{1,2},{2,3},{3,0},{4,5},{5,6},{6,7},{7,4},{8,9},{9,10},{10,1... | collective-permute-start | bytes 98312 | tf_op jit(solution)/shard_map/ppermute | solution.py:29
  50.8 17.9 %all-to-all-start = ((f32[32,64,128]{2,0,1:T(8,128)}), f32[32,64,128]{2,0,1:T(8,128)S(1)}, u32[]{:S(2)}, u32[]{:S(2)}) async-start(f32[32,64,128]{2,0,1:T(8,128)} %bitcast.16), calls=%async_computation | async-start | bytes 2097152 | tf_op jit(solution)/shard_map/all_to_all | solution.py:76
  54.4 46.5 %reduce-scatter.3.cloned.1.call-start = ((), (), s32[]{:S(2)}) async-start(), calls=%async_computation.5 | async-start | bytes 1310720 | tf_op jit(solution)/shard_map/reduce_scatter | solution.py:104
  57.1 0.7 copy-start.4
  57.8 0.7 copy-start.2
  68.8 0.8 copy-start
  73.1 55.9 %all-gather.2.cloned.1.call-start = ((), (), s32[]{:S(2)}) async-start(), calls=%async_computation.6 | async-start | bytes 1310720 | tf_op jit(solution)/shard_map/all_gather | solution.py:108
  100.9 124.4 %reduce-scatter.5.cloned.1.call-start = ((), (), s32[]{:S(2)}) async-start(), calls=%async_computation.7 | async-start | bytes 1310720 | tf_op jit(solution)/shard_map/reduce_scatter | solution.py:104
  101.9 28.8 %copy-start.1 = (f32[128,128]{1,0:T(8,128)S(1)}, f32[128,128]{1,0:T(8,128)}, u32[]{:S(2)}) copy-start(f32[128,128]{1,0:T(8,128)} %constant.60.clone) | copy-start | bytes 196612
  151.0 1.7 collective-permute-start.9
  151.0 3.4 %collective-permute-start.8 = (f32[1,2,8,4,128]{4,0,3,2,1:T(1,128)S(1)}, f32[1,2,8,4,128]{4,0,3,2,1:T(1,128)S(1)}, u32[]{:S(2)}, u32[]{:S(2)}) collective-permute-start(f32[1,2,8,4,128]{4,0,3,2,1:T(1,128)S(1)} %bitcast.81), channel_id=1, source_target_pairs={{0,1},{1,2},{2,3},{3,0},{4,5},{5,6},{6,7},{7,4},{8,9},{9,10},{10,1... | collective-permute-start | bytes 98312 | tf_op jit(solution)/shard_map/ppermute | solution.py:29
  158.1 1.7 collective-permute-start.11
  158.2 3.4 %collective-permute-start.10 = (f32[1,2,8,4,128]{4,0,3,2,1:T(1,128)S(1)}, f32[1,2,8,4,128]{4,0,3,2,1:T(1,128)S(1)}, u32[]{:S(2)}, u32[]{:S(2)}) collective-permute-start(f32[1,2,8,4,128]{4,0,3,2,1:T(1,128)S(1)} %get-tuple-element.51), channel_id=1, source_target_pairs={{0,1},{1,2},{2,3},{3,0},{4,5},{5,6},{6,7},{7,4},{8,9},{9,10},{10,1... | collective-permute-start | bytes 98312 | tf_op jit(solution)/shard_map/ppermute | solution.py:29
  165.3 1.7 collective-permute-start.13
  165.4 3.6 %collective-permute-start.12 = (f32[1,2,8,4,128]{4,0,3,2,1:T(1,128)S(1)}, f32[1,2,8,4,128]{4,0,3,2,1:T(1,128)S(1)}, u32[]{:S(2)}, u32[]{:S(2)}) collective-permute-start(f32[1,2,8,4,128]{4,0,3,2,1:T(1,128)S(1)} %get-tuple-element.35), channel_id=1, source_target_pairs={{0,1},{1,2},{2,3},{3,0},{4,5},{5,6},{6,7},{7,4},{8,9},{9,10},{10,1... | collective-permute-start | bytes 98312 | tf_op jit(solution)/shard_map/ppermute | solution.py:29
  172.7 1.7 collective-permute-start.15
  172.7 3.4 %collective-permute-start.14 = (f32[1,2,8,4,128]{4,0,3,2,1:T(1,128)S(1)}, f32[1,2,8,4,128]{4,0,3,2,1:T(1,128)S(1)}, u32[]{:S(2)}, u32[]{:S(2)}) collective-permute-start(f32[1,2,8,4,128]{4,0,3,2,1:T(1,128)S(1)} %get-tuple-element.19), channel_id=1, source_target_pairs={{0,1},{1,2},{2,3},{3,0},{4,5},{5,6},{6,7},{7,4},{8,9},{9,10},{10,1... | collective-permute-start | bytes 98312 | tf_op jit(solution)/shard_map/ppermute | solution.py:29
Sparse Core Ops, SparseCore 0:
  73.2 27.6 reduce-scatter.2
  102.4 26.4 all-gather.1
  199.5 25.7 reduce-scatter.4
where the time goes:
time: 232 us
  waiting for transfers between devices  112 us (48%)
  blocking collectives  33.8 us (15%)
  between operations  25.4 us (11%)
  local copies, waits for them, and re-layouts  24.6 us (11%)
  other arithmetic  20.2 us (9%)
  starting transfers between devices  11.5 us (5%)
  matrix products  3.88 us (2%)
    reduce_scatter x2, waiting for transfers between devices, reduce_terms(): lax.psum_scatter(terms[owner], 'grid', scatter_dimension=0, tiled=True)  53.7 us
    all_gather x1, waiting for transfers between devices, local(): ordered = lax.all_gather(summed, 'grid', axis=0, tiled=True)  27 us
    add x8, other arithmetic, advance(): return centre + change  19.2 us
    all_to_all x1, blocking collectives, local(): lax.all_to_all(nodal, 'slab', split_axis=0, concat_axis=1, tiled=True)  17 us
    all_to_all x1, blocking collectives, regroup_rows(): lax.all_to_all(stepped, 'slab', split_axis=1, concat_axis=0, tiled=True)  16.9 us
    ppermute x8, waiting for transfers between devices, extended_2(): before = lax.ppermute(last, axis, up)  12.5 us
    slice x56, local copies, waits for them, and re-layouts, advance(): back = jnp.roll(centre, 1, axis)  10.6 us
    all_to_all x1, waiting for transfers between devices, regroup_rows(): lax.all_to_all(stepped, 'slab', split_axis=1, concat_axis=0, tiled=True)  10.3 us
  transfers between devices with their start and end apart: 20, of which 18 were waited for; matrix products, arithmetic and copies ran while one was open for 2% of the time, Pallas kernels for 0%

commit v1 on v0

v1 whole, which is shorter than its diff:
```python
import functools
import math

import jax
import jax.numpy as jnp
from jax import lax
from jax.experimental import pallas as pl
from jax.experimental.pallas import tpu as pltpu
from jax.sharding import PartitionSpec as P

N1 = 2
N2 = 8
N3 = 4
STEPS = 4
SUB = 8
CHUNK = 2
LOW = STEPS
HIGH = STEPS + 1

ADVECT = 0.08
DIFFUSE = 0.03
MESH = pl.DeviceIdType.MESH


def advance_row(u, back0, ahead0, coef):
    adv, dif, adv_sum, dif_sum = coef
    tiles = u.shape[0]
    sub = lax.broadcasted_iota(jnp.int32, u.shape, 1)
    inner = sub % N3
    back3 = jnp.where(inner == 0, pltpu.roll(u, SUB - N3 + 1, 1), pltpu.roll(u, 1, 1))
    ahead3 = jnp.where(inner == N3 - 1, pltpu.roll(u, N3 - 1, 1), pltpu.roll(u, SUB - 1, 1))
    turned = pltpu.roll(u, N3, 1)
    half = tiles // N1
    parts = [turned[n * half:(n + 1) * half] for n in range(N1)]
    before = jnp.concatenate([x for p in parts for x in (p[half - 1:], p[:half - 1])], axis=0)
    after = jnp.concatenate([x for p in parts for x in (p[1:], p[:1])], axis=0)
    back2 = jnp.where(sub < N3, before, turned)
    ahead2 = jnp.where(sub < N3, turned, after)
    other = jnp.concatenate([u[half:], u[:half]], axis=0)
    back4 = pltpu.roll(u, 1, 2)
    ahead4 = pltpu.roll(u, u.shape[2] - 1, 2)
    upwind = (adv[0] * back0 + adv[1] * other + adv[2] * back2 + adv[3] * back3 + adv[4] * back4
              - adv_sum * u)
    spread = (dif[0] * (back0 + ahead0) + (2.0 * dif[1]) * other + dif[2] * (back2 + ahead2)
              + dif[3] * (back3 + ahead3) + dif[4] * (back4 + ahead4) - dif_sum * u)
    return u + (1.0 + 0.5 * jnp.tanh(u)) * upwind + spread


def kernel(sizes, par, owner, u_in, out, ext_a, ext_b, ext_s, terms, from_left, from_right,
           final, whole, rs_left, rs_right, rs_send,
           h_send, h_recv, up_send, l_recv, r_recv, dl_send, dr_send, d_recv, g_send, g_recv,
           a_send, a_recv, rs_ssem, rsl_recv, rsr_recv):
    Z, S, rows, count = sizes
    z = lax.axis_index("grid")
    s = lax.axis_index("slab")
    nxt, prv = lax.rem(s + 1, S), lax.rem(s + S - 1, S)
    ext = rows + LOW + HIGH
    chunks = rows // CHUNK
    pairs = chunks // 2
    tiles_out = whole.shape[1]
    owned = count // Z
    piece = rs_left.shape[2]
    pieces = owned // piece

    def remote(src, dst, ssem, rsem, **where):
        return pltpu.make_async_remote_copy(src_ref=src, dst_ref=dst, send_sem=ssem, recv_sem=rsem,
                                            device_id=where, device_id_type=MESH)

    adv = [par[d] for d in range(5)]
    dif = [par[5 + d] for d in range(5)]
    coef = (adv, dif, par[10], par[11])
    weight, keep_mid, keep_fine = par[12], par[13], par[14]

    barrier = pltpu.get_barrier_semaphore()
    for off in range(1, S):
        pl.semaphore_signal(barrier, inc=1, device_id={"slab": lax.rem(s + off, S)}, device_id_type=MESH)

    @pl.when(z > 0)
    def _():
        pl.semaphore_signal(barrier, inc=1, device_id={"grid": z - 1}, device_id_type=MESH)

    @pl.when(z < Z - 1)
    def _():
        pl.semaphore_signal(barrier, inc=1, device_id={"grid": z + 1}, device_id_type=MESH)

    pl.semaphore_wait(barrier, S - 1 + jnp.where(z > 0, 1, 0) + jnp.where(z < Z - 1, 1, 0))

    def run_rows(src, dst, low, high):
        @pl.loop(low, high)
        def _(e):
            dst[e] = advance_row(src[e], src[e - 1], src[e + 1], coef)

    def later_steps():
        run_rows(ext_b, ext_a, 2, ext - 2)
        run_rows(ext_a, ext_b, 3, ext - 3)
        run_rows(ext_b, ext_a, 4, ext - 4)

    def make_terms(dst):
        @pl.loop(0, rows // 4)
        def _(m):
            r = 4 * m
            u0, u1, u2, u3, u4 = [ext_a[LOW + r + k] for k in range(5)]
            dst[r] = weight * u0
            dst[r + 1] = (weight * keep_fine) * (u1 - 0.5 * (u0 + u2))
            dst[r + 2] = (weight * keep_mid) * (u2 - 0.5 * (u0 + u4))
            dst[r + 3] = (weight * keep_fine) * (u3 - 0.5 * (u2 + u4))

    up = remote(u_in.at[pl.ds(rows - LOW, LOW)], ext_a.at[pl.ds(0, LOW)], h_send.at[0], h_recv.at[0], slab=nxt)
    down = remote(u_in.at[pl.ds(0, HIGH)], ext_a.at[pl.ds(LOW + rows, HIGH)], h_send.at[1], h_recv.at[1], slab=prv)
    up.start()
    down.start()

    @pl.loop(0, rows)
    def _(r):
        ext_a[LOW + r] = u_in[r]

    run_rows(ext_a, ext_b, LOW + 1, LOW + rows - 1)
    up.wait()
    down.wait()
    run_rows(ext_a, ext_b, 1, LOW + 1)
    run_rows(ext_a, ext_b, LOW + rows - 1, ext - 1)
    later_steps()
    make_terms(terms)

    roots = (Z // 2 - 1, Z // 2)

    def at(position):
        return lax.rem(position + chunks - 2, chunks)

    def span(c):
        return pl.ds(c * CHUNK, CHUNK)

    def shifted(c):
        return pl.ds(LOW + c * CHUNK, CHUNK)

    def to_right(c):
        return remote(terms.at[span(c)], from_left.at[span(c)], up_send.at[c], l_recv.at[c], grid=lax.rem(z + 1, Z))

    def to_left(c):
        return remote(terms.at[span(c)], from_right.at[span(c)], up_send.at[c], r_recv.at[c],
                      grid=lax.rem(z + Z - 1, Z))

    def result_right(c):
        return remote(ext_s.at[shifted(c)], ext_s.at[shifted(c)], dr_send.at[c], d_recv.at[c], grid=lax.rem(z + 1, Z))

    def result_left(c):
        return remote(ext_s.at[shifted(c)], ext_s.at[shifted(c)], dl_send.at[c], d_recv.at[c],
                      grid=lax.rem(z + Z - 1, Z))

    def add_in(c, other):
        for k in range(CHUNK):
            terms[c * CHUNK + k] += other[c * CHUNK + k]

    def inward(c, root):
        @pl.when(z < root)
        def _():
            @pl.when(z > 0)
            def _():
                to_right(c).wait_recv()
                add_in(c, from_left)
            to_right(c).start()

        @pl.when(z > root)
        def _():
            @pl.when(z < Z - 1)
            def _():
                to_left(c).wait_recv()
                add_in(c, from_right)
            to_left(c).start()

    def at_root(c, root):
        @pl.when(z == root)
        def _():
            if root > 0:
                to_right(c).wait_recv()
                add_in(c, from_left)
            if root < Z - 1:
                to_left(c).wait_recv()
                add_in(c, from_right)
            for k in range(CHUNK):
                ext_s[LOW + c * CHUNK + k] = terms[c * CHUNK + k]
            if root > 0:
                result_left(c).start()
            if root < Z - 1:
                result_right(c).start()

    def outward(c, root):
        @pl.when(z < root)
        def _():
            result_right(c).wait_recv()

            @pl.when(z > 0)
            def _():
                result_left(c).start()

        @pl.when(z > root)
        def _():
            result_left(c).wait_recv()

            @pl.when(z < Z - 1)
            def _():
                result_right(c).start()

    halo_up = remote(ext_s.at[pl.ds(rows, LOW)], ext_s.at[pl.ds(0, LOW)], g_send.at[0], g_recv.at[0], slab=nxt)
    halo_down = remote(ext_s.at[pl.ds(LOW, HIGH)], ext_s.at[pl.ds(LOW + rows, HIGH)], g_send.at[1], g_recv.at[1],
                       slab=prv)
    root_lag, out_lag = 1, 2
    edge = out_lag + (4 + CHUNK + HIGH) // (2 * CHUNK)

    @pl.loop(0, pairs + out_lag)
    def _(j):
        @pl.when(j < pairs)
        def _():
            for k, root in enumerate(roots):
                inward(at(2 * j + k), root)

        @pl.when((j >= root_lag) & (j < pairs + root_lag))
        def _():
            for k, root in enumerate(roots):
                at_root(at(2 * (j - root_lag) + k), root)

        @pl.when(j >= out_lag)
        def _():
            for k, root in enumerate(roots):
                outward(at(2 * (j - out_lag) + k), root)

        @pl.when(j == edge)
        def _():
            halo_up.start()
            halo_down.start()

    def restart(low, high):
        @pl.loop(low, high)
        def _(m):
            e = 4 * m
            s0, s1, s2, s3, s4 = [ext_s[e + k] for k in range(5)]
            mid = 0.5 * (s0 + s4) + keep_mid * s2
            ext_a[e] = s0
            ext_a[e + 1] = 0.5 * (s0 + mid) + keep_fine * s1
            ext_a[e + 2] = mid
            ext_a[e + 3] = 0.5 * (mid + s4) + keep_fine * s3
            ext_a[e + 4] = s4

    halo_up.wait()
    halo_down.wait()
    restart(0, (ext - 1) // 4)
    run_rows(ext_a, ext_b, 1, ext - 1)
    later_steps()
    make_terms(final)

    def exchange(off):
        peer = lax.rem(s + off, S)
        return remote(final.at[:, pl.ds(peer * tiles_out, tiles_out)], whole.at[pl.ds(s * rows, rows)],
                      a_send.at[off - 1], a_recv.at[off - 1], slab=peer)

    def arrival(off):
        peer = lax.rem(s + S - off, S)
        return remote(final.at[:, pl.ds(peer * tiles_out, tiles_out)], whole.at[pl.ds(peer * rows, rows)],
                      a_send.at[off - 1], a_recv.at[off - 1], slab=peer)

    for off in range(1, S):
        exchange(off).start()

    @pl.loop(0, rows)
    def _(r):
        whole[s * rows + r] = final[r, pl.ds(s * tiles_out, tiles_out)]

    @pl.loop(0, chunks)
    def _(c):
        for k, root in enumerate(roots):
            @pl.when((lax.rem(c + 2, chunks) % 2 == k) & (z != root))
            def _():
                to_right(c).wait_send()

            @pl.when((lax.rem(c + 2, chunks) % 2 == k) & (z <= root) & (z > 0))
            def _():
                result_left(c).wait_send()

            @pl.when((lax.rem(c + 2, chunks) % 2 == k) & (z >= root) & (z < Z - 1))
            def _():
                result_right(c).wait_send()

    for off in range(1, S):
        arrival(off).wait_recv()
    for spacing in [1 << t for t in range(2, count.bit_length() - 1)]:
        for i in range(spacing, count, 2 * spacing):
            whole[i] = whole[i] - 0.5 * (whole[i - spacing] + whole[(i + spacing) % count])

    def rs_right_copy(k, p):
        return remote(rs_send.at[k, p], rs_left.at[k, p], rs_ssem.at[k, p], rsl_recv.at[k, p], grid=lax.rem(z + 1, Z))

    def rs_left_copy(k, p):
        return remote(rs_send.at[k, p], rs_right.at[k, p], rs_ssem.at[k, p], rsr_recv.at[k, p],
                      grid=lax.rem(z + Z - 1, Z))

    def own(k, p, r):
        return whole[owner[k * owned + p * piece + r]]

    @pl.loop(0, (Z - 1) * pieces)
    def _(j):
        p = j % pieces
        k = Z - 1 - j // pieces

        @pl.when(k > z)
        def _():
            @pl.loop(0, piece)
            def _(r):
                rs_send[k, p, r] = own(k, p, r)

            @pl.when(z > 0)
            def _():
                rs_right_copy(k, p).wait_recv()

                @pl.loop(0, piece)
                def _(r):
                    rs_send[k, p, r] += rs_left[k, p, r]
            rs_right_copy(k, p).start()

        n = j // pieces

        @pl.when(n < z)
        def _():
            @pl.loop(0, piece)
            def _(r):
                rs_send[n, p, r] = own(n, p, r)

            @pl.when(z < Z - 1)
            def _():
                rs_left_copy(n, p).wait_recv()

                @pl.loop(0, piece)
                def _(r):
                    rs_send[n, p, r] += rs_right[n, p, r]
            rs_left_copy(n, p).start()

    @pl.loop(0, pieces)
    def _(p):
        @pl.loop(0, piece)
        def _(r):
            out[p * piece + r] = own(z, p, r)

        @pl.when(z > 0)
        def _():
            rs_right_copy(z, p).wait_recv()

            @pl.loop(0, piece)
            def _(r):
                out[p * piece + r] += rs_left[z, p, r]

        @pl.when(z < Z - 1)
        def _():
            rs_left_copy(z, p).wait_recv()

            @pl.loop(0, piece)
            def _(r):
                out[p * piece + r] += rs_right[z, p, r]

    for off in range(1, S):
        exchange(off).wait_send()

    @pl.loop(0, Z)
    def _(k):
        @pl.when(k != z)
        def _():
            @pl.loop(0, pieces)
            def _(p):
                rs_right_copy(k, p).wait_send()


def local(field, levels, owner):
    _, rows, flat, lanes = field.shape
    Z, S = lax.axis_size("grid"), lax.axis_size("slab")
    count = owner.shape[0]
    tiles = flat // SUB
    tiles_out = tiles // S
    owned = count // Z
    piece = min(owned, 8)
    ext = rows + LOW + HIGH
    chunks = rows // CHUNK
    depth = count.bit_length() - 1
    vec = levels[0]
    scales = jnp.exp2(vec.astype(jnp.float32)) / 8.0
    adv = ADVECT * scales
    dif = DIFFUSE * scales ** 2
    weight = jnp.where(jnp.sum(vec) % 2 == 0, 1.0, -1.0) / math.sqrt(Z)
    kept = [(depth - t <= depth - 3 + vec[0]).astype(jnp.float32) for t in (1, 0)]
    par = jnp.concatenate([adv, dif, jnp.stack([jnp.sum(adv), 2.0 * jnp.sum(dif), weight.astype(jnp.float32), *kept])])
    u = field[0].reshape(rows, tiles, SUB, lanes)
    tail = (tiles, SUB, lanes)
    tail_out = (tiles_out, SUB, lanes)
    f32 = jnp.float32
    vmem = lambda *shape: pltpu.VMEM(shape, f32)
    sems = lambda *shape: pltpu.SemaphoreType.DMA(shape)
    pieces = owned // piece
    result = pl.pallas_call(
        functools.partial(kernel, (Z, S, rows, count)),
        out_shape=jax.ShapeDtypeStruct((owned,) + tail_out, f32),
        in_specs=[pl.BlockSpec(memory_space=pltpu.SMEM), pl.BlockSpec(memory_space=pltpu.SMEM),
                  pl.BlockSpec(memory_space=pltpu.VMEM)],
        out_specs=pl.BlockSpec(memory_space=pltpu.VMEM),
        scratch_shapes=[
            vmem(ext, *tail), vmem(ext, *tail), vmem(ext, *tail),
            vmem(rows, *tail), vmem(rows, *tail), vmem(rows, *tail),
            vmem(rows, *tail), vmem(count, *tail_out),
            vmem(Z, pieces, piece, *tail_out), vmem(Z, pieces, piece, *tail_out), vmem(Z, pieces, piece, *tail_out),
            sems(2), sems(2), sems(chunks), sems(chunks), sems(chunks), sems(chunks), sems(chunks), sems(chunks),
            sems(2), sems(2), sems(S - 1), sems(S - 1),
            sems(Z, pieces), sems(Z, pieces), sems(Z, pieces),
        ],
        compiler_params=pltpu.CompilerParams(collective_id=0, has_side_effects=True,
                                             vmem_limit_bytes=40 * 1024 * 1024),
    )(par, owner, u)
    return result.reshape(owned, flat // S, lanes)


def solution(mesh):
    in_specs = (P(("copies", "grid"), "slab", None, None), P(("copies", "grid"), None), P("copies"))
    out_specs = P(("copies", "grid"), "slab", None)
    return jax.shard_map(local, mesh=mesh, in_specs=in_specs, out_specs=out_specs, check_vma=False)
```

time: 232 us -> 147 us (0.63)
  Pallas kernels: 0 us -> 140 us
  waiting for transfers between devices: 112 us -> 0 us
  blocking collectives: 33.8 us -> 0 us
  between operations: 25.4 us -> 2.68 us
  local copies, waits for them, and re-layouts: 24.6 us -> 3.37 us
  other arithmetic: 20.2 us -> 1.33 us
  starting transfers between devices: 11.5 us -> 0 us
  matrix products: 3.88 us -> 0 us
    pallas_call x0 -> x1, Pallas kernels: none -> 140 us  [local(): pl.pallas_call(functools.partial(kernel, (Z, S, rows, count)), out_shape=...]
    reduce_scatter x2 -> x0, waiting for transfers between devices: 53.7 us -> none  [reduce_terms(): lax.psum_scatter(terms[owner], 'grid', scatter_dimension=0, tiled=True)]
    all_to_all x2 -> x0, blocking collectives: 33.8 us -> none  [the longest x1 17 us: local(): lax.all_to_all(nodal, 'slab', split_axis=0, concat_axis=1, tiled=True)]
    all_gather x1 -> x0, waiting for transfers between devices: 27 us -> none  [local(): ordered = lax.all_gather(summed, 'grid', axis=0, tiled=True)]
    ppermute x16 -> x0, waiting for transfers between devices: 21.4 us -> none  [the longest x8 12.5 us: extended_2(): before = lax.ppermute(last, axis, up)]
    add x8 -> x0, other arithmetic: 19.2 us -> none  [advance(): return centre + change]
    slice x65 -> x0, local copies, waits for them, and re-layouts: 12.3 us -> none  [the longest x56 10.6 us: advance(): back = jnp.roll(centre, 1, axis)]
    all_to_all x1 -> x0, waiting for transfers between devices: 10.3 us -> none  [regroup_rows(): lax.all_to_all(stepped, 'slab', split_axis=1, concat_axis=0, tiled=True)]
  transfers between devices with their start and end apart: 20 -> 0, of which waited for: 18 -> 0; matrix products, arithmetic and copies ran while one was open for 2% -> 0% of each run, Pallas kernels for 0% -> 0%
where the time goes in v1:
time: 147 us
  Pallas kernels  140 us (95%)
  local copies, waits for them, and re-layouts  3.37 us (2%)
  between operations  2.68 us (2%)
    pallas_call x1, Pallas kernels, local(): pl.pallas_call(functools.partial(kernel, (Z, S, rows, count)), out_shape=...  140 us

profile of v1, /device:TPU:0, one launch (start us, length us, event | category | flops | bytes accessed | tf_op | source)
XLA Modules:
  0.0 146.9 jit_solution(10732317186858891926)
XLA Ops:
  0.0 0.0 copy-start.2
  0.0 0.7 copy-done.2
  0.7 0.6 reduce_sum.29
  3.3 0.7 fusion
  4.6 0.0 copy-start.1
  4.7 0.8 concatenate.3.par
  5.4 0.0 copy-done.1
  5.4 0.0 copy-start
  5.4 1.2 copy-done
  6.7 139.5 %shard_map.37 = f32[32,2,8,128]{3,2,1,0:T(8,128)S(1)} custom-call(f32[15]{0:T(128)S(1)} %concatenate.3.par, s32[128]{0:T(128)S(1)} %copy-done.1, f32[32,8,8,128]{3,2,1,0:T(8,128)S(1)} %bitcast.12), custom_call_target="tpu_custom_call" | custom-call | tf_op jit(solution)/shard_map/pallas_call | solution.py:395
  146.2 0.7 copy.5
Async XLA Ops:
  0.0 0.7 copy-start.2
  4.6 0.8 copy-start.1
  5.4 1.2 copy-start

commit v2 on v1

--- a/solution.py
+++ b/solution.py
@@ -14,6 +14,9 @@
 STEPS = 4
 SUB = 8
 CHUNK = 2
+ROOT_LAG = 2
+OUT_LAG = 5
+RS_LAG = 2
 LOW = STEPS
 HIGH = STEPS + 1
 
@@ -46,10 +49,10 @@
     return u + (1.0 + 0.5 * jnp.tanh(u)) * upwind + spread
 
 
-def kernel(sizes, par, owner, u_in, out, ext_a, ext_b, ext_s, terms, from_left, from_right,
+def kernel(sizes, levels, owner, u_in, out, ext_a, ext_b, ext_s, terms, from_left, from_right,
            final, whole, rs_left, rs_right, rs_send,
            h_send, h_recv, up_send, l_recv, r_recv, dl_send, dr_send, d_recv, g_send, g_recv,
-           a_send, a_recv, rs_ssem, rsl_recv, rsr_recv):
+           a_send, a_recv, rs_ssem, rsl_recv, rsr_recv, in_sem):
     Z, S, rows, count = sizes
     z = lax.axis_index("grid")
     s = lax.axis_index("slab")
@@ -66,10 +69,16 @@
         return pltpu.make_async_remote_copy(src_ref=src, dst_ref=dst, send_sem=ssem, recv_sem=rsem,
                                             device_id=where, device_id_type=MESH)
 
-    adv = [par[d] for d in range(5)]
-    dif = [par[5 + d] for d in range(5)]
-    coef = (adv, dif, par[10], par[11])
-    weight, keep_mid, keep_fine = par[12], par[13], par[14]
+    loaded = pltpu.make_async_copy(u_in, ext_a.at[pl.ds(LOW, rows)], in_sem)
+    loaded.start()
+    vec = [levels[0, d] for d in range(5)]
+    scales = [lax.shift_left(jnp.int32(1), v).astype(jnp.float32) * 0.125 for v in vec]
+    adv = [ADVECT * x for x in scales]
+    dif = [DIFFUSE * (x * x) for x in scales]
+    coef = (adv, dif, sum(adv[1:], adv[0]), 2.0 * sum(dif[1:], dif[0]))
+    size = jnp.float32(1.0 / math.sqrt(Z))
+    weight = jnp.where(sum(vec[1:], vec[0]) % 2 == 0, size, -size)
+    keep_mid, keep_fine = [jnp.where(3 - t <= vec[0], jnp.float32(1.0), jnp.float32(0.0)) for t in (1, 0)]
 
     barrier = pltpu.get_barrier_semaphore()
     for off in range(1, S):
@@ -105,14 +114,11 @@
             dst[r + 2] = (weight * keep_mid) * (u2 - 0.5 * (u0 + u4))
             dst[r + 3] = (weight * keep_fine) * (u3 - 0.5 * (u2 + u4))
 
-    up = remote(u_in.at[pl.ds(rows - LOW, LOW)], ext_a.at[pl.ds(0, LOW)], h_send.at[0], h_recv.at[0], slab=nxt)
-    down = remote(u_in.at[pl.ds(0, HIGH)], ext_a.at[pl.ds(LOW + rows, HIGH)], h_send.at[1], h_recv.at[1], slab=prv)
+    up = remote(ext_a.at[pl.ds(rows, LOW)], ext_a.at[pl.ds(0, LOW)], h_send.at[0], h_recv.at[0], slab=nxt)
+    loaded.wait()
+    down = remote(ext_a.at[pl.ds(LOW, HIGH)], ext_a.at[pl.ds(LOW + rows, HIGH)], h_send.at[1], h_recv.at[1], slab=prv)
     up.start()
     down.start()
-
-    @pl.loop(0, rows)
-    def _(r):
-        ext_a[LOW + r] = u_in[r]
 
     run_rows(ext_a, ext_b, LOW + 1, LOW + rows - 1)
     up.wait()
@@ -125,7 +131,7 @@
     roots = (Z // 2 - 1, Z // 2)
 
     def at(position):
-        return lax.rem(position + chunks - 2, chunks)
+        return lax.rem(position + chunks - LOW // CHUNK, chunks)
 
     def span(c):
         return pl.ds(c * CHUNK, CHUNK)
@@ -204,8 +210,8 @@
     halo_up = remote(ext_s.at[pl.ds(rows, LOW)], ext_s.at[pl.ds(0, LOW)], g_send.at[0], g_recv.at[0], slab=nxt)
     halo_down = remote(ext_s.at[pl.ds(LOW, HIGH)], ext_s.at[pl.ds(LOW + rows, HIGH)], g_send.at[1], g_recv.at[1],
                        slab=prv)
-    root_lag, out_lag = 1, 2
-    edge = out_lag + (4 + CHUNK + HIGH) // (2 * CHUNK)
+    root_lag, out_lag = ROOT_LAG, OUT_LAG
+    edge = out_lag + (LOW // CHUNK + -(-HIGH // CHUNK) - 1) // 2
 
     @pl.loop(0, pairs + out_lag)
     def _(j):
@@ -268,15 +274,15 @@
     @pl.loop(0, chunks)
     def _(c):
         for k, root in enumerate(roots):
-            @pl.when((lax.rem(c + 2, chunks) % 2 == k) & (z != root))
+            @pl.when(((c + LOW // CHUNK) % 2 == k) & (z != root))
             def _():
                 to_right(c).wait_send()
 
-            @pl.when((lax.rem(c + 2, chunks) % 2 == k) & (z <= root) & (z > 0))
+            @pl.when(((c + LOW // CHUNK) % 2 == k) & (z <= root) & (z > 0))
             def _():
                 result_left(c).wait_send()
 
-            @pl.when((lax.rem(c + 2, chunks) % 2 == k) & (z >= root) & (z < Z - 1))
+            @pl.when(((c + LOW // CHUNK) % 2 == k) & (z >= root) & (z < Z - 1))
             def _():
                 result_right(c).wait_send()
 
@@ -296,12 +302,17 @@
     def own(k, p, r):
         return whole[owner[k * owned + p * piece + r]]
 
-    @pl.loop(0, (Z - 1) * pieces)
+    steps = (Z - 1) * pieces
+
+    @pl.loop(0, steps + (Z - 1) * RS_LAG)
     def _(j):
-        p = j % pieces
-        k = Z - 1 - j // pieces
-
-        @pl.when(k > z)
+        jr = j - RS_LAG * z
+        inside_r = (jr >= 0) & (jr < steps)
+        jr = jnp.clip(jr, 0, steps - 1)
+        p = jr % pieces
+        k = Z - 1 - jr // pieces
+
+        @pl.when(inside_r & (k > z))
         def _():
             @pl.loop(0, piece)
             def _(r):
@@ -316,22 +327,26 @@
                     rs_send[k, p, r] += rs_left[k, p, r]
             rs_right_copy(k, p).start()
 
-        n = j // pieces
-
-        @pl.when(n < z)
+        jl = j - RS_LAG * (Z - 1 - z)
+        inside_l = (jl >= 0) & (jl < steps)
+        jl = jnp.clip(jl, 0, steps - 1)
+        q = jl % pieces
+        n = jl // pieces
+
+        @pl.when(inside_l & (n < z))
         def _():
             @pl.loop(0, piece)
             def _(r):
-                rs_send[n, p, r] = own(n, p, r)
+                rs_send[n, q, r] = own(n, q, r)
 
             @pl.when(z < Z - 1)
             def _():
-                rs_left_copy(n, p).wait_recv()
+                rs_left_copy(n, q).wait_recv()
 
                 @pl.loop(0, piece)
                 def _(r):
-                    rs_send[n, p, r] += rs_right[n, p, r]
-            rs_left_copy(n, p).start()
+                    rs_send[n, q, r] += rs_right[n, q, r]
+            rs_left_copy(n, q).start()
 
     @pl.loop(0, pieces)
     def _(p):
@@ -377,14 +392,6 @@
     piece = min(owned, 8)
     ext = rows + LOW + HIGH
     chunks = rows // CHUNK
-    depth = count.bit_length() - 1
-    vec = levels[0]
-    scales = jnp.exp2(vec.astype(jnp.float32)) / 8.0
-    adv = ADVECT * scales
-    dif = DIFFUSE * scales ** 2
-    weight = jnp.where(jnp.sum(vec) % 2 == 0, 1.0, -1.0) / math.sqrt(Z)
-    kept = [(depth - t <= depth - 3 + vec[0]).astype(jnp.float32) for t in (1, 0)]
-    par = jnp.concatenate([adv, dif, jnp.stack([jnp.sum(adv), 2.0 * jnp.sum(dif), weight.astype(jnp.float32), *kept])])
     u = field[0].reshape(rows, tiles, SUB, lanes)
     tail = (tiles, SUB, lanes)
     tail_out = (tiles_out, SUB, lanes)
@@ -396,7 +403,7 @@
         functools.partial(kernel, (Z, S, rows, count)),
         out_shape=jax.ShapeDtypeStruct((owned,) + tail_out, f32),
         in_specs=[pl.BlockSpec(memory_space=pltpu.SMEM), pl.BlockSpec(memory_space=pltpu.SMEM),
-                  pl.BlockSpec(memory_space=pltpu.VMEM)],
+                  pl.BlockSpec(memory_space=pl.ANY)],
         out_specs=pl.BlockSpec(memory_space=pltpu.VMEM),
         scratch_shapes=[
             vmem(ext, *tail), vmem(ext, *tail), vmem(ext, *tail),
@@ -405,11 +412,11 @@
             vmem(Z, pieces, piece, *tail_out), vmem(Z, pieces, piece, *tail_out), vmem(Z, pieces, piece, *tail_out),
             sems(2), sems(2), sems(chunks), sems(chunks), sems(chunks), sems(chunks), sems(chunks), sems(chunks),
             sems(2), sems(2), sems(S - 1), sems(S - 1),
-            sems(Z, pieces), sems(Z, pieces), sems(Z, pieces),
+            sems(Z, pieces), sems(Z, pieces), sems(Z, pieces), pltpu.SemaphoreType.DMA,
         ],
         compiler_params=pltpu.CompilerParams(collective_id=0, has_side_effects=True,
                                              vmem_limit_bytes=40 * 1024 * 1024),
-    )(par, owner, u)
+    )(levels, owner, u)
     return result.reshape(owned, flat // S, lanes)
 
 

time: 147 us -> 109 us (0.74)
  Pallas kernels: 140 us -> 105 us
  between operations: 2.68 us -> 0.01 us
    pallas_call x1, Pallas kernels: 140 us -> 105 us  [local(): pl.pallas_call(functools.partial(kernel, (Z, S, rows, count)), out_shape=...]
where the time goes in v2:
time: 109 us; the launch traced here: 108 us
  Pallas kernels  105 us (96%)
  local copies, waits for them, and re-layouts  2.6 us (2%)
    pallas_call x1, Pallas kernels, local(): pl.pallas_call(functools.partial(kernel, (Z, S, rows, count)), out_shape=...  105 us
    unnamed x7, local copies, waits for them, and re-layouts  2.6 us

profile of v2, /device:TPU:0, one launch (start us, length us, event | category | flops | bytes accessed | tf_op | source)
XLA Modules:
  0.0 107.6 jit_solution(8903458915545982899)
XLA Ops:
  0.0 0.0 copy-start.2
  0.0 0.0 copy-start.1
  0.0 0.7 copy-done.2
  0.7 0.0 copy-done.1
  0.7 0.0 copy-start
  0.7 1.2 %copy-done = f32[1,32,64,128]{3,2,1,0:T(8,128)S(1)} copy-done((f32[1,32,64,128]{3,2,1,0:T(8,128)S(1)}, f32[1,32,64,128]{3,2,1,0:T(8,128)}, u32[]{:S(2)}) %copy-start) | copy-done | bytes 1048600
  1.9 105.0 %shard_map.37 = f32[32,2,8,128]{3,2,1,0:T(8,128)S(1)} custom-call(s32[1,5]{1,0:T(1,128)S(1)} %copy-done.1, s32[128]{0:T(128)S(1)} %copy-done.2, f32[32,8,8,128]{3,2,1,0:T(8,128)S(1)} %bitcast.2), custom_call_target="tpu_custom_call" | custom-call | tf_op jit(solution)/shard_map/pallas_call | solution.py:402
  106.9 0.7 copy.5
Async XLA Ops:
  0.0 0.7 copy-start.2
  0.0 0.7 copy-start.1
  0.7 1.2 %copy-start = (f32[1,32,64,128]{3,2,1,0:T(8,128)S(1)}, f32[1,32,64,128]{3,2,1,0:T(8,128)}, u32[]{:S(2)}) copy-start(f32[1,32,64,128]{3,2,1,0:T(8,128)} %param.3) | copy-start | bytes 3145732

commit v3 on v2

--- a/solution.py
+++ b/solution.py
@@ -17,6 +17,7 @@
 ROOT_LAG = 2
 OUT_LAG = 5
 RS_LAG = 2
+WAVE_LAG = 4
 LOW = STEPS
 HIGH = STEPS + 1
 
@@ -49,7 +50,7 @@
     return u + (1.0 + 0.5 * jnp.tanh(u)) * upwind + spread
 
 
-def kernel(sizes, levels, owner, u_in, out, ext_a, ext_b, ext_s, terms, from_left, from_right,
+def kernel(sizes, levels, owner, u_in, out, first, second, ext_s, terms, from_left, from_right,
            final, whole, rs_left, rs_right, rs_send,
            h_send, h_recv, up_send, l_recv, r_recv, dl_send, dr_send, d_recv, g_send, g_recv,
            a_send, a_recv, rs_ssem, rsl_recv, rsr_recv, in_sem):
@@ -69,7 +70,8 @@
         return pltpu.make_async_remote_copy(src_ref=src, dst_ref=dst, send_sem=ssem, recv_sem=rsem,
                                             device_id=where, device_id_type=MESH)
 
-    loaded = pltpu.make_async_copy(u_in, ext_a.at[pl.ds(LOW, rows)], in_sem)
+    groups = rows // 4
+    loaded = pltpu.make_async_copy(u_in, first.at[0, pl.ds(LOW, rows)], in_sem)
     loaded.start()
     vec = [levels[0, d] for d in range(5)]
     scales = [lax.shift_left(jnp.int32(1), v).astype(jnp.float32) * 0.125 for v in vec]
@@ -94,39 +96,30 @@
 
     pl.semaphore_wait(barrier, S - 1 + jnp.where(z > 0, 1, 0) + jnp.where(z < Z - 1, 1, 0))
 
-    def run_rows(src, dst, low, high):
-        @pl.loop(low, high)
-        def _(e):
-            dst[e] = advance_row(src[e], src[e - 1], src[e + 1], coef)
-
-    def later_steps():
-        run_rows(ext_b, ext_a, 2, ext - 2)
-        run_rows(ext_a, ext_b, 3, ext - 3)
-        run_rows(ext_b, ext_a, 4, ext - 4)
-
-    def make_terms(dst):
-        @pl.loop(0, rows // 4)
-        def _(m):
-            r = 4 * m
-            u0, u1, u2, u3, u4 = [ext_a[LOW + r + k] for k in range(5)]
-            dst[r] = weight * u0
-            dst[r + 1] = (weight * keep_fine) * (u1 - 0.5 * (u0 + u2))
-            dst[r + 2] = (weight * keep_mid) * (u2 - 0.5 * (u0 + u4))
-            dst[r + 3] = (weight * keep_fine) * (u3 - 0.5 * (u2 + u4))
-
-    up = remote(ext_a.at[pl.ds(rows, LOW)], ext_a.at[pl.ds(0, LOW)], h_send.at[0], h_recv.at[0], slab=nxt)
+    def wave(bufs, g, fresh):
+        for k in range(1, STEPS + 1):
+            low = jnp.where(fresh, 4 * g + k, 4 * g + 9 - k)
+
+            @pl.loop(low, 4 * g + 13 - k)
+            def _(e):
+                bufs[k, e] = advance_row(bufs[k - 1, e], bufs[k - 1, e - 1], bufs[k - 1, e + 1], coef)
+
+    def make_terms(bufs, g, dst):
+        r = 4 * g
+        u0, u1, u2, u3, u4 = [bufs[STEPS, LOW + r + k] for k in range(5)]
+        dst[r] = weight * u0
+        dst[r + 1] = (weight * keep_fine) * (u1 - 0.5 * (u0 + u2))
+        dst[r + 2] = (weight * keep_mid) * (u2 - 0.5 * (u0 + u4))
+        dst[r + 3] = (weight * keep_fine) * (u3 - 0.5 * (u2 + u4))
+
+    up = remote(first.at[0, pl.ds(rows, LOW)], first.at[0, pl.ds(0, LOW)], h_send.at[0], h_recv.at[0], slab=nxt)
     loaded.wait()
-    down = remote(ext_a.at[pl.ds(LOW, HIGH)], ext_a.at[pl.ds(LOW + rows, HIGH)], h_send.at[1], h_recv.at[1], slab=prv)
+    down = remote(first.at[0, pl.ds(LOW, HIGH)], first.at[0, pl.ds(LOW + rows, HIGH)], h_send.at[1], h_recv.at[1], slab=prv)
     up.start()
     down.start()
 
-    run_rows(ext_a, ext_b, LOW + 1, LOW + rows - 1)
     up.wait()
     down.wait()
-    run_rows(ext_a, ext_b, 1, LOW + 1)
-    run_rows(ext_a, ext_b, LOW + rows - 1, ext - 1)
-    later_steps()
-    make_terms(terms)
 
     roots = (Z // 2 - 1, Z // 2)
 
@@ -213,10 +206,38 @@
     root_lag, out_lag = ROOT_LAG, OUT_LAG
     edge = out_lag + (LOW // CHUNK + -(-HIGH // CHUNK) - 1) // 2
 
-    @pl.loop(0, pairs + out_lag)
+    def restart(m):
+        e = 4 * m
+        s0, s1, s2, s3, s4 = [ext_s[e + k] for k in range(5)]
+        mid = 0.5 * (s0 + s4) + keep_mid * s2
+        second[0, e] = s0
+        second[0, e + 1] = 0.5 * (s0 + mid) + keep_fine * s1
+        second[0, e + 2] = mid
+        second[0, e + 3] = 0.5 * (mid + s4) + keep_fine * s3
+        second[0, e + 4] = s4
+
+    def exchange(off, g):
+        peer = lax.rem(s + off, S)
+        return remote(final.at[pl.ds(4 * g, 4), pl.ds(peer * tiles_out, tiles_out)],
+                      whole.at[pl.ds(s * rows + 4 * g, 4)],
+                      a_send.at[off - 1, g], a_recv.at[off - 1, g], slab=peer)
+
+    def arrival(off, g):
+        peer = lax.rem(s + S - off, S)
+        return remote(final.at[pl.ds(4 * g, 4), pl.ds(peer * tiles_out, tiles_out)],
+                      whole.at[pl.ds(peer * rows + 4 * g, 4)],
+                      a_send.at[off - 1, g], a_recv.at[off - 1, g], slab=peer)
+
+    last = pairs + out_lag
+    wave_lag = out_lag + WAVE_LAG
+
+    @pl.loop(0, max(last, groups + wave_lag))
     def _(j):
         @pl.when(j < pairs)
         def _():
+            g = lax.rem(j + groups - 1, groups)
+            wave(first, g, j < 2)
+            make_terms(first, g, terms)
             for k, root in enumerate(roots):
                 inward(at(2 * j + k), root)
 
@@ -225,7 +246,7 @@
             for k, root in enumerate(roots):
                 at_root(at(2 * (j - root_lag) + k), root)
 
-        @pl.when(j >= out_lag)
+        @pl.when((j >= out_lag) & (j < last))
         def _():
             for k, root in enumerate(roots):
                 outward(at(2 * (j - out_lag) + k), root)
@@ -235,41 +256,23 @@
             halo_up.start()
             halo_down.start()
 
-    def restart(low, high):
-        @pl.loop(low, high)
-        def _(m):
-            e = 4 * m
-            s0, s1, s2, s3, s4 = [ext_s[e + k] for k in range(5)]
-            mid = 0.5 * (s0 + s4) + keep_mid * s2
-            ext_a[e] = s0
-            ext_a[e + 1] = 0.5 * (s0 + mid) + keep_fine * s1
-            ext_a[e + 2] = mid
-            ext_a[e + 3] = 0.5 * (mid + s4) + keep_fine * s3
-            ext_a[e + 4] = s4
-
-    halo_up.wait()
-    halo_down.wait()
-    restart(0, (ext - 1) // 4)
-    run_rows(ext_a, ext_b, 1, ext - 1)
-    later_steps()
-    make_terms(final)
-
-    def exchange(off):
-        peer = lax.rem(s + off, S)
-        return remote(final.at[:, pl.ds(peer * tiles_out, tiles_out)], whole.at[pl.ds(s * rows, rows)],
-                      a_send.at[off - 1], a_recv.at[off - 1], slab=peer)
-
-    def arrival(off):
-        peer = lax.rem(s + S - off, S)
-        return remote(final.at[:, pl.ds(peer * tiles_out, tiles_out)], whole.at[pl.ds(peer * rows, rows)],
-                      a_send.at[off - 1], a_recv.at[off - 1], slab=peer)
-
-    for off in range(1, S):
-        exchange(off).start()
-
-    @pl.loop(0, rows)
-    def _(r):
-        whole[s * rows + r] = final[r, pl.ds(s * tiles_out, tiles_out)]
+        @pl.when(j == wave_lag)
+        def _():
+            halo_up.wait()
+            halo_down.wait()
+            restart(0)
+            restart(1)
+
+        @pl.when((j >= wave_lag) & (j < groups + wave_lag))
+        def _():
+            g = j - wave_lag
+            restart(g + 2)
+            wave(second, g, g == 0)
+            make_terms(second, g, final)
+            for off in range(1, S):
+                exchange(off, g).start()
+            for k in range(4):
+                whole[s * rows + 4 * g + k] = final[4 * g + k, pl.ds(s * tiles_out, tiles_out)]
 
     @pl.loop(0, chunks)
     def _(c):
@@ -286,8 +289,11 @@
             def _():
                 result_right(c).wait_send()
 
-    for off in range(1, S):
-        arrival(off).wait_recv()
+    @pl.loop(0, groups)
+    def _(g):
+        for off in range(1, S):
+            arrival(off, g).wait_recv()
+
     for spacing in [1 << t for t in range(2, count.bit_length() - 1)]:
         for i in range(spacing, count, 2 * spacing):
             whole[i] = whole[i] - 0.5 * (whole[i - spacing] + whole[(i + spacing) % count])
@@ -370,8 +376,10 @@
             def _(r):
                 out[p * piece + r] += rs_right[z, p, r]
 
-    for off in range(1, S):
-        exchange(off).wait_send()
+    @pl.loop(0, groups)
+    def _(g):
+        for off in range(1, S):
+            exchange(off, g).wait_send()
 
     @pl.loop(0, Z)
     def _(k):
@@ -406,12 +414,12 @@
                   pl.BlockSpec(memory_space=pl.ANY)],
         out_specs=pl.BlockSpec(memory_space=pltpu.VMEM),
         scratch_shapes=[
-            vmem(ext, *tail), vmem(ext, *tail), vmem(ext, *tail),
+            vmem(STEPS + 1, ext, *tail), vmem(STEPS + 1, ext, *tail), vmem(ext, *tail),
             vmem(rows, *tail), vmem(rows, *tail), vmem(rows, *tail),
             vmem(rows, *tail), vmem(count, *tail_out),
             vmem(Z, pieces, piece, *tail_out), vmem(Z, pieces, piece, *tail_out), vmem(Z, pieces, piece, *tail_out),
             sems(2), sems(2), sems(chunks), sems(chunks), sems(chunks), sems(chunks), sems(chunks), sems(chunks),
-            sems(2), sems(2), sems(S - 1), sems(S - 1),
+            sems(2), sems(2), sems(S - 1, rows // 4), sems(S - 1, rows // 4),
             sems(Z, pieces), sems(Z, pieces), sems(Z, pieces), pltpu.SemaphoreType.DMA,
         ],
         compiler_params=pltpu.CompilerParams(collective_id=0, has_side_effects=True,

time: 109 us -> 97.5 us (0.89); the launches traced: 108 us -> 97.3 us
  Pallas kernels: 105 us -> 94.7 us
    pallas_call x1, Pallas kernels: 105 us -> 94.7 us  [local(): pl.pallas_call(functools.partial(kernel, (Z, S, rows, count)), out_shape=...]
where the time goes in v3:
time: 97.5 us; the launch traced here: 97.3 us
  Pallas kernels  94.7 us (97%)
  local copies, waits for them, and re-layouts  2.6 us (3%)
    pallas_call x1, Pallas kernels, local(): pl.pallas_call(functools.partial(kernel, (Z, S, rows, count)), out_shape=...  94.7 us
    unnamed x7, local copies, waits for them, and re-layouts  2.6 us

profile of v3, /device:TPU:0, one launch (start us, length us, event | category | flops | bytes accessed | tf_op | source)
XLA Modules:
  0.0 97.3 jit_solution(9805548315547220575)
XLA Ops:
  0.0 0.0 copy-start.2
  0.0 0.0 copy-start.1
  0.0 0.7 copy-done.2
  0.7 0.0 copy-done.1
  0.7 0.0 copy-start
  0.7 1.2 %copy-done = f32[1,32,64,128]{3,2,1,0:T(8,128)S(1)} copy-done((f32[1,32,64,128]{3,2,1,0:T(8,128)S(1)}, f32[1,32,64,128]{3,2,1,0:T(8,128)}, u32[]{:S(2)}) %copy-start) | copy-done | bytes 1048600
  1.9 94.7 %shard_map.37 = f32[32,2,8,128]{3,2,1,0:T(8,128)S(1)} custom-call(s32[1,5]{1,0:T(1,128)S(1)} %copy-done.1, s32[128]{0:T(128)S(1)} %copy-done.2, f32[32,8,8,128]{3,2,1,0:T(8,128)S(1)} %bitcast.2), custom_call_target="tpu_custom_call" | custom-call | tf_op jit(solution)/shard_map/pallas_call | solution.py:410
  96.6 0.7 copy.5
Async XLA Ops:
  0.0 0.7 copy-start.2
  0.0 0.7 copy-start.1
  0.7 1.2 %copy-start = (f32[1,32,64,128]{3,2,1,0:T(8,128)S(1)}, f32[1,32,64,128]{3,2,1,0:T(8,128)}, u32[]{:S(2)}) copy-start(f32[1,32,64,128]{3,2,1,0:T(8,128)} %param.3) | copy-start | bytes 3145732

commit v4 on v3

--- a/solution.py
+++ b/solution.py
@@ -14,10 +14,10 @@
 STEPS = 4
 SUB = 8
 CHUNK = 2
-ROOT_LAG = 2
-OUT_LAG = 5
+ROOT_LAG = 3
+OUT_LAG = 7
 RS_LAG = 2
-WAVE_LAG = 4
+WAVE_LAG = 3
 LOW = STEPS
 HIGH = STEPS + 1
 
@@ -100,9 +100,14 @@
         for k in range(1, STEPS + 1):
             low = jnp.where(fresh, 4 * g + k, 4 * g + 9 - k)
 
-            @pl.loop(low, 4 * g + 13 - k)
+            @pl.loop(low, 4 * g + 9 - k)
             def _(e):
                 bufs[k, e] = advance_row(bufs[k - 1, e], bufs[k - 1, e - 1], bufs[k - 1, e + 1], coef)
+
+            @pl.loop(0, 2)
+            def _(n):
+                for e in [4 * g + 9 - k + 2 * n + i for i in range(2)]:
+                    bufs[k, e] = advance_row(bufs[k - 1, e], bufs[k - 1, e - 1], bufs[k - 1, e + 1], coef)
 
     def make_terms(bufs, g, dst):
         r = 4 * g

time: 97.5 us -> 86.7 us (0.89)
  Pallas kernels: 94.7 us -> 83.9 us
    pallas_call x1, Pallas kernels: 94.7 us -> 83.9 us  [local(): pl.pallas_call(functools.partial(kernel, (Z, S, rows, count)), out_shape=...]
where the time goes in v4:
time: 86.7 us; the launch traced here: 86.5 us
  Pallas kernels  83.9 us (97%)
  local copies, waits for them, and re-layouts  2.6 us (3%)
    pallas_call x1, Pallas kernels, local(): pl.pallas_call(functools.partial(kernel, (Z, S, rows, count)), out_shape=...  83.9 us
    unnamed x7, local copies, waits for them, and re-layouts  2.6 us

profile of v4, /device:TPU:0, one launch (start us, length us, event | category | flops | bytes accessed | tf_op | source)
XLA Modules:
  0.0 86.5 jit_solution(4121697384663152898)
XLA Ops:
  0.0 0.0 copy-start.2
  0.0 0.0 copy-start.1
  0.0 0.7 copy-done.2
  0.7 0.0 copy-done.1
  0.7 0.0 copy-start
  0.7 1.2 %copy-done = f32[1,32,64,128]{3,2,1,0:T(8,128)S(1)} copy-done((f32[1,32,64,128]{3,2,1,0:T(8,128)S(1)}, f32[1,32,64,128]{3,2,1,0:T(8,128)}, u32[]{:S(2)}) %copy-start) | copy-done | bytes 1048600
  1.9 83.9 %shard_map.37 = f32[32,2,8,128]{3,2,1,0:T(8,128)S(1)} custom-call(s32[1,5]{1,0:T(1,128)S(1)} %copy-done.1, s32[128]{0:T(128)S(1)} %copy-done.2, f32[32,8,8,128]{3,2,1,0:T(8,128)S(1)} %bitcast.2), custom_call_target="tpu_custom_call" | custom-call | tf_op jit(solution)/shard_map/pallas_call | solution.py:415
  85.8 0.7 copy.5
Async XLA Ops:
  0.0 0.7 copy-start.2
  0.0 0.7 copy-start.1
  0.7 1.2 %copy-start = (f32[1,32,64,128]{3,2,1,0:T(8,128)S(1)}, f32[1,32,64,128]{3,2,1,0:T(8,128)}, u32[]{:S(2)}) copy-start(f32[1,32,64,128]{3,2,1,0:T(8,128)} %param.3) | copy-start | bytes 3145732
